TPU v7x, 256 devices: a whole 4x4x8 slice. The times are simulated.
256 devices in a mesh: worker: 16 (over y, x_hi, core), mp: 16 (over z, x_lo).
Axes of the slice: x: 4 (x_hi: 2, x_lo: 2; x = x_hi * 2 + x_lo), y: 4, z: 8, core: 2. Of those that a mesh axis runs over, the one named last changes fastest.
Arguments:
- gradients: float32 [16, 8388608], P('worker', 'mp'), may hold values from -100 to 100
- neighbours: int32 [16, 11], replicated, may hold values from 0 to 15, as said below
- winner: int32 [1], replicated, may hold values from 0 to 15
Outputs:
- scores: float32 [16], replicated
- aggregate: float32 [8388608], P(('mp', 'worker'))
Inputs may be any that keep to these rules, and one draw needn't show every extreme that they name: `neighbours`: row i lists 11 different workers, none of them equal to i.
All inputs are finite; a program needn't handle non-finite values.
Results may differ from a plain program's by a relative error of at most 0.0003.
Values may be sent and summed in bfloat16 or wider, within the bound.
A program may use at most 64 MiB of HBM per device.

v0:
```python
import jax
import jax.numpy as jnp
from jax import lax
from jax.sharding import Mesh
from jax.sharding import PartitionSpec as P

WORKER = ("worker_0", "worker_1", "worker_2")
WORKER_MP = ("worker_0", "worker_1", "worker_2", "mp_0", "mp_1")
MP = ("mp_0", "mp_1")
MP_WORKER = ("mp_0", "mp_1", "worker_0", "worker_1", "worker_2")


def one_axis_at_a_time(shard, axes):
    for axis in axes:
        shard = lax.psum(shard, axis)
    return shard


def split_up(shard, dim, length):
    before, after = (shard.shape[:dim], shard.shape[dim + 1 :])
    return jnp.moveaxis(shard.reshape(*before, length, -1, *after), dim, 0)


def sent_and_summed(shard, axis, dim):
    length = lax.axis_size(axis)
    parts = lax.all_to_all(split_up(shard, dim, length), axis, 0, 0, tiled=True)
    return jnp.sum(parts, axis=0)


def body(gradients, neighbours, winner):
    rounded = gradients.astype(jnp.bfloat16)
    workers = lax.axis_size(WORKER)
    own_index = lax.axis_index(WORKER)
    length = gradients.shape[1]
    columns = lax.all_to_all(rounded, WORKER, split_axis=1, concat_axis=0, tiled=True)
    partial_value = lax.dot_general(
        columns, columns, (((1,), (1,)), ((), ())), preferred_element_type=jnp.float32
    )
    gram_matrix = one_axis_at_a_time(partial_value, WORKER_MP)
    squares = jnp.diagonal(gram_matrix)
    distance = squares[:, None] + squares[None, :] - 2.0 * gram_matrix
    counts = jnp.sum(
        (neighbours[:, :, None] == jnp.arange(workers, dtype=jnp.int32)[None, None, :]).astype(
            jnp.float32
        ),
        axis=1,
    )
    total_entries = neighbours.shape[1] * length * lax.axis_size(MP)
    scores = jnp.sum(counts * distance, axis=1) / jnp.float32(total_entries)
    is_owner = (own_index == winner[0]).astype(jnp.float32)
    own_shard = gradients[0]
    aggregate = sent_and_summed(is_owner * own_shard, WORKER, 0)
    return (scores, aggregate)


def solution(mesh):
    split = Mesh(
        mesh.devices.reshape(4, 2, 2, 8, 2), ("worker_0", "worker_1", "worker_2", "mp_0", "mp_1")
    )
    in_specs = (P(WORKER, MP), P(), P())
    out_specs = (P(), P(MP_WORKER))
    return jax.shard_map(body, mesh=split, in_specs=in_specs, out_specs=out_specs, check_vma=False)
```

profile of v0, /device:TPU:6, one launch (start us, length us, event | category | flops | bytes accessed | tf_op | source)
XLA Modules:
  0.0 111.8 jit_solution(10468273172557672134)
XLA Ops:
  1.3 6.1 %broadcast_multiply_fusion = (f32[1,524288]{1,0:T(1,128)}, bf16[1,524288]{1,0:T(2,128)(2,1)S(1)}) fusion(f32[1,524288]{1,0:T(1,128)} %param.3, f32[]{:T(128)S(6)} %convert_element_type.11), kind=kLoop, calls=%fused_computation.4 | loop fusion | flops 1048576 | bytes 5242884 | tf_op jit(solution)/shard_map/mul | solution.py:52
  7.4 0.5 broadcast.40
  7.9 7.0 %reduce.1 = bf16[16,32768]{1,0:T(8,128)(2,1)S(1)} reduce(bf16[16,1,32768]{2,1,0:T(2,128)(2,1)S(1)} %bitcast.11, bf16[]{:T(256)} %broadcast.40), dimensions={1}, to_apply=%bitcast.8.reduce_sub_computation | reduce | bytes 2097154
  14.9 0.8 reshape.35
  15.7 22.6 %all_to_all.22 = bf16[16,2,16384]{2,1,0:T(2,128)(2,1)S(1)} all-to-all(bf16[16,2,16384]{2,1,0:T(2,128)(2,1)S(1)} %reshape.35), channel_id=1, replica_groups=mesh['worker_0'=4,'worker_1'=2,'worker_2'=2,'mp_0'=8,'mp_1'=2] {'worker_..., dimensions={0} | all-to-all | bytes 2097152 | tf_op jit(solution)/shard_map/all_to_all | solution.py:35
  38.3 0.0 copy-start
  38.3 6.4 %all-to-all-start.1 = ((f32[16,1,32768]{2,1,0:T(1,128)}), f32[16,1,32768]{2,1,0:T(1,128)S(1)}, u32[]{:S(2)}, u32[]{:S(2)}) async-start(f32[16,1,32768]{2,1,0:T(1,128)} %bitcast.3), calls=%async_computation.1 | async-start | bytes 4194304 | tf_op jit(solution)/shard_map/all_to_all | solution.py:26
  44.7 0.0 copy-done
  44.7 0.1 copy.5
  44.8 0.1 convert_reduce_fusion
  44.9 3.5 %reshape.36 = bf16[16,1,32768]{2,1,0:T(2,128)(2,1)} reshape(bf16[16,2,16384]{2,1,0:T(2,128)(2,1)S(1)} %all_to_all.22) | data formatting | bytes 2097152
  48.4 4.5 %fusion = f32[16,16]{1,0:T(8,128)S(1)} fusion(bf16[1,16,32768]{2,0,1:T(2,128)(2,1)} %bitcast.12), kind=kOutput, calls=%fused_computation.1 | convolution fusion | flops 16777216 | bytes 1049600 | tf_op jit(solution)/shard_map/dot_general | solution.py:36
  52.8 20.9 %psum.35 = f32[16,16]{1,0:T(8,128)S(1)} all-reduce(f32[16,16]{1,0:T(8,128)S(1)} %fusion), channel_id=1, replica_groups=mesh['worker_0'=4,'worker_1'=2,'worker_2'=2,'mp_0'=8,'mp_1'=2] {'worker_0'}, use_global_device_ids=true, to_apply=%region_1.0 | all-reduce | flops 256 | bytes 2048 | tf_op jit(solution)/shard_map/psum | solution.py:15
  73.8 6.5 %psum.36 = f32[16,16]{1,0:T(8,128)S(1)} all-reduce(f32[16,16]{1,0:T(8,128)S(1)} %psum.35), channel_id=1, replica_groups=mesh['worker_0'=4,'worker_1'=2,'worker_2'=2,'mp_0'=8,'mp_1'=2] {'worker_1'}, use_global_device_ids=true, to_apply=%region_2.0 | all-reduce | flops 256 | bytes 2048 | tf_op jit(solution)/shard_map/psum | solution.py:15
  80.3 2.5 %psum.37 = f32[16,16]{1,0:T(8,128)S(1)} all-reduce(f32[16,16]{1,0:T(8,128)S(1)} %psum.36), channel_id=1, replica_groups=mesh['worker_0'=4,'worker_1'=2,'worker_2'=2,'mp_0'=8,'mp_1'=2] {'worker_2'}, use_global_device_ids=true, to_apply=%region_3.0 | all-reduce | flops 256 | bytes 2048 | tf_op jit(solution)/shard_map/psum | solution.py:15
  82.8 20.2 %psum.38 = f32[16,16]{1,0:T(8,128)S(1)} all-reduce(f32[16,16]{1,0:T(8,128)S(1)} %psum.37), channel_id=1, replica_groups=mesh['worker_0'=4,'worker_1'=2,'worker_2'=2,'mp_0'=8,'mp_1'=2] {'mp_0'}, use_global_device_ids=true, to_apply=%region_4.0 | all-reduce | flops 256 | bytes 2048 | tf_op jit(solution)/shard_map/psum | solution.py:15
  103.0 5.0 %psum.39 = f32[16,16]{1,0:T(8,128)S(1)} all-reduce(f32[16,16]{1,0:T(8,128)S(1)} %psum.38), channel_id=1, replica_groups=mesh['worker_0'=4,'worker_1'=2,'worker_2'=2,'mp_0'=8,'mp_1'=2] {'mp_1'}, use_global_device_ids=true, to_apply=%region_5.6 | all-reduce | flops 256 | bytes 2048 | tf_op jit(solution)/shard_map/psum | solution.py:15
  108.0 0.7 gather_fusion
  108.7 0.2 multiply_reduce_fusion
  108.9 0.5 broadcast_multiply_fusion.1
  109.4 0.0 all-to-all-done.1
  109.4 2.4 %reduce_sum.29 = f32[32768]{0:T(1024)} reduce(f32[16,1,32768]{2,1,0:T(1,128)S(1)} %all-to-all-done.1, f32[]{:T(128)} %constant.10.clone.1), dimensions={0,1}, to_apply=%region_7.8 | reduce | flops 491520 | bytes 2228228 | tf_op jit(solution)/shard_map/reduce_sum | solution.py:27
  (1 shorter events, 0.0 us)
Async XLA Ops:
  38.3 6.4 %copy-start = (s32[16,11]{1,0:T(8,128)S(1)}, s32[16,11]{1,0:T(8,128)}, u32[]{:S(2)}) copy-start(s32[16,11]{1,0:T(8,128)} %param.4) | copy-start | bytes 2116
  38.3 71.1 %all-to-all-start.1 = ((f32[16,1,32768]{2,1,0:T(1,128)}), f32[16,1,32768]{2,1,0:T(1,128)S(1)}, u32[]{:S(2)}, u32[]{:S(2)}) async-start(f32[16,1,32768]{2,1,0:T(1,128)} %bitcast.3), calls=%async_computation.1 | async-start | bytes 4194304 | tf_op jit(solution)/shard_map/all_to_all | solution.py:26
where the time goes:
time: 112 us
  blocking collectives  77.7 us (69%)
  other arithmetic  16.3 us (15%)
  starting transfers between devices  6.38 us (6%)
  local copies, waits for them, and re-layouts  5.57 us (5%)
  matrix products  4.49 us (4%)
  between operations  1.33 us (1%)
    psum x5, blocking collectives, one_axis_at_a_time(): shard = lax.psum(shard, axis)  55.2 us
    all_to_all x1, blocking collectives, body(): lax.all_to_all(rounded, WORKER, split_axis=1, concat_axis=0, tiled=True)  22.6 us
    unnamed x1, other arithmetic  7.02 us
    all_to_all x1, starting transfers between devices, sent_and_summed(): parts = lax.all_to_all(split_up(shard, dim, length), axis, 0, 0, tiled=True)  6.38 us
    mul x1, other arithmetic, body(): aggregate = sent_and_summed(is_owner * own_shard, WORKER, 0)  6.08 us
    unnamed x6, local copies, waits for them, and re-layouts  4.91 us
    dot_general x1, matrix products, body(): lax.dot_general(columns, columns, (((1,), (1,)), ((), ())), preferred_ele...  4.49 us
    reduce_sum x1, other arithmetic, sent_and_summed(): return jnp.sum(parts, axis=0)  2.39 us
  transfers between devices with their start and end apart: 1, of which 0 were waited for; matrix products, arithmetic and copies ran while one was open for 9% of the time, Pallas kernels for 0%

commit v1 on v0

v1 whole, which is shorter than its diff:
```python
import functools

import jax
import jax.numpy as jnp
from jax import lax
from jax.experimental import pallas as pl
from jax.experimental.pallas import tpu as pltpu
from jax.sharding import Mesh
from jax.sharding import PartitionSpec as P

AXES = ("y", "xh", "c", "z", "xl")
WORKER = ("y", "xh", "c")
MP = ("z", "xl")
MP_WORKER = ("z", "xl", "y", "xh", "c")
MESH = pl.DeviceIdType.MESH

WORKERS = 16
ROWS = 256
HALF = ROWS // 2
LANES = 128

CHIPS = [(2, 2), (2, 0), (0, 2), (2, 1), (0, 1), (2, 3), (0, 3)]
PEERS = [(dx, dy, 0, c) for dx, dy in CHIPS for c in (0, 1)] + [(0, 0, 0, 1)]
LINE = [(0, 0, dz, 0) for dz in (4, 3, 5, 2, 6, 1, 7)]
PLANE = [
    (dx, dy, 0, c)
    for dx, dy in sorted(
        ((a, b) for a in range(4) for b in range(4)),
        key=lambda p: -(min(p[0], 4 - p[0]) + min(p[1], 4 - p[1])),
    )
    for c in (0, 1)
    if (dx, dy, c) != (0, 0, 0)
]


def place():
    x = lax.axis_index("xh") * 2 + lax.axis_index("xl")
    return x, lax.axis_index("y"), lax.axis_index("z"), lax.axis_index("c")


def at_offset(offset):
    x, y, z, c = (
        lax.rem(own + step, size) for own, step, size in zip(place(), offset, (4, 4, 8, 2))
    )
    return x, y, z, c


def device(offset):
    x, y, z, c = at_offset(offset)
    return {"y": y, "xh": x // 2, "c": c, "z": z, "xl": lax.rem(x, 2)}


def chip_index(offset):
    x, y, _, _ = at_offset(offset)
    return y * 2 + x // 2


def worker_index(offset):
    return chip_index(offset) * 2 + at_offset(offset)[3]


def send(src, dst, send_sem, recv_sem, offset):
    copy = pltpu.make_async_remote_copy(
        src_ref=src,
        dst_ref=dst,
        send_sem=send_sem,
        recv_sem=recv_sem,
        device_id=device(offset),
        device_id_type=MESH,
    )
    copy.start()
    return copy


def wait_bytes(ref, sem):
    pltpu.make_async_copy(ref, ref, sem).wait()


def kernel(
    total_entries,
    winner_ref,
    neighbours_ref,
    gradients_ref,
    scores_ref,
    aggregate_ref,
    full,
    hi,
    lo,
    lo_away,
    lo_mine,
    lo_got,
    got,
    gram,
    line_src,
    line_got,
    plane_src,
    plane_got,
    load_sem,
    hi_send,
    hi_recv,
    lo_send,
    lo_recv,
    sum_send,
    sum_recv,
):
    own_core = lax.axis_index("c")
    own_chip = chip_index((0, 0, 0, 0))
    own = worker_index((0, 0, 0, 0))
    winner = winner_ref[0]

    order = PEERS + [(0, 0, 0, 0)]
    loads = []
    for slot, offset in enumerate(order):
        rows = pl.ds(pl.multiple_of(worker_index(offset) * ROWS, ROWS), ROWS)
        load = pltpu.make_async_copy(gradients_ref.at[rows], full.at[slot], load_sem.at[slot])
        load.start()
        loads.append(load)

    barrier = pltpu.get_barrier_semaphore()
    partners = LINE + PLANE
    for offset in partners:
        pl.semaphore_signal(barrier, inc=1, device_id=device(offset), device_id_type=MESH)

    for slot, offset in enumerate(order):
        loads[slot].wait()
        value = full[slot]
        high = value.astype(jnp.bfloat16)
        low = (value - high.astype(jnp.float32)).astype(jnp.bfloat16)
        if slot < len(PEERS):
            hi[slot] = high
        else:
            got[own] = high
        if offset[3] == 0:
            lo[own_core, chip_index(offset)] = low
        else:
            lo_away[chip_index(offset)] = low

    pl.semaphore_wait(barrier, len(partners))

    copies = []
    for half in range(2):
        rows = pl.ds(half * HALF, HALF)
        for slot, offset in enumerate(PEERS):
            copies.append(
                send(
                    hi.at[slot, rows],
                    got.at[own, rows],
                    hi_send.at[half],
                    hi_recv.at[half],
                    offset,
                )
            )
    swap = send(lo_away, lo.at[own_core], lo_send.at[0], lo_recv.at[0], (0, 0, 0, 1))

    row = lax.broadcasted_iota(jnp.int32, (WORKERS, ROWS), 0)
    column = lax.broadcasted_iota(jnp.int32, (WORKERS, ROWS), 1) // 16
    counts = jnp.zeros((WORKERS, ROWS), jnp.float32)
    number = neighbours_ref.shape[1]
    for entry in range(number):
        counts += (neighbours_ref[:, entry : entry + 1] == column).astype(jnp.float32)
    line_src[...] = jnp.zeros_like(line_src)

    swap.wait()
    lo_mine[...] = lo[lax.rem(winner, 2)]

    def product(half):
        parts = [
            got[:, pl.ds(half * HALF + step * 16, 16), :].reshape(ROWS, LANES)
            for step in range(HALF // 16)
        ]
        block = jnp.concatenate(parts, axis=1)
        return lax.dot_general(
            block, block, (((1,), (1,)), ((), ())), preferred_element_type=jnp.float32
        )

    wait_bytes(got.at[pl.ds(0, 15), pl.ds(0, HALF)], hi_recv.at[0])
    gram[...] = product(0)
    wait_bytes(got.at[pl.ds(0, 15), pl.ds(0, HALF)], hi_recv.at[1])

    for dx, dy in CHIPS:
        offset = (dx, dy, 0, 0)
        send(
            lo_mine.at[chip_index(offset)],
            lo_got.at[own_chip],
            lo_send.at[1],
            lo_recv.at[1],
            offset,
        )
    lo_got[own_chip] = lo_mine[own_chip]

    total = gram[...] + product(1)
    sublane = lax.broadcasted_iota(jnp.int32, (ROWS, ROWS), 0)
    lane = lax.broadcasted_iota(jnp.int32, (ROWS, ROWS), 1)
    total = jnp.where(lax.rem(sublane, 16) == lax.rem(lane, 16), total, 0.0)
    total = jnp.sum(total.reshape(WORKERS, 16, ROWS), axis=1)
    diagonal = jnp.where(row == column, total, 0.0)
    squares = jnp.sum(diagonal, axis=0, keepdims=True)
    own_counts = jnp.sum(counts, axis=1, keepdims=True) * (1.0 / 16.0)
    partial = counts * (squares - 2.0 * total) + own_counts * diagonal
    partial = lax.dot_general(
        jnp.ones((8, ROWS), jnp.float32),
        partial,
        (((1,), (1,)), ((), ())),
        precision=lax.Precision.HIGHEST,
        preferred_element_type=jnp.float32,
    )
    line_src[:, pl.ds(0, WORKERS)] = partial[0:1]

    for step, offset in enumerate(LINE):
        send(line_src, line_got.at[step], sum_send.at[0], sum_recv.at[0], offset)
    wait_bytes(line_got, sum_recv.at[0])
    plane_src[...] = line_src[...] + jnp.sum(line_got[...], axis=0)
    for step, offset in enumerate(PLANE):
        send(plane_src, plane_got.at[step], sum_send.at[1], sum_recv.at[1], offset)

    wait_bytes(lo_got.at[pl.ds(0, 7)], lo_recv.at[1])
    aggregate_ref[...] = got[winner].astype(jnp.float32) + lo_got[winner // 2].astype(jnp.float32)

    wait_bytes(plane_got, sum_recv.at[1])
    scores = (plane_src[...] + jnp.sum(plane_got[...], axis=0)) / jnp.float32(total_entries)
    scores_ref[...] = scores

    for half in range(2):
        wait_bytes(got.at[pl.ds(0, 15), pl.ds(0, HALF)], hi_send.at[half])
    wait_bytes(lo_got.at[pl.ds(0, 7)], lo_send.at[1])
    wait_bytes(line_got, sum_send.at[0])
    wait_bytes(plane_got, sum_send.at[1])


def body(gradients, neighbours, winner):
    length = gradients.shape[1]
    total_entries = neighbours.shape[1] * length * lax.axis_size(MP)
    bf16, f32 = jnp.bfloat16, jnp.float32
    scores, aggregate = pl.pallas_call(
        functools.partial(kernel, total_entries),
        out_shape=(
            jax.ShapeDtypeStruct((1, LANES), f32),
            jax.ShapeDtypeStruct((ROWS, LANES), f32),
        ),
        in_specs=[
            pl.BlockSpec(memory_space=pltpu.SMEM),
            pl.BlockSpec(memory_space=pltpu.VMEM),
            pl.BlockSpec(memory_space=pl.ANY),
        ],
        out_specs=(
            pl.BlockSpec(memory_space=pltpu.VMEM),
            pl.BlockSpec(memory_space=pltpu.VMEM),
        ),
        scratch_shapes=[
            pltpu.VMEM((16, ROWS, LANES), f32),
            pltpu.VMEM((15, ROWS, LANES), bf16),
            pltpu.VMEM((2, 8, ROWS, LANES), bf16),
            pltpu.VMEM((8, ROWS, LANES), bf16),
            pltpu.VMEM((8, ROWS, LANES), bf16),
            pltpu.VMEM((8, ROWS, LANES), bf16),
            pltpu.VMEM((16, ROWS, LANES), bf16),
            pltpu.VMEM((ROWS, ROWS), f32),
            pltpu.VMEM((1, LANES), f32),
            pltpu.VMEM((len(LINE), 1, LANES), f32),
            pltpu.VMEM((1, LANES), f32),
            pltpu.VMEM((len(PLANE), 1, LANES), f32),
            pltpu.SemaphoreType.DMA((16,)),
            pltpu.SemaphoreType.DMA((2,)),
            pltpu.SemaphoreType.DMA((2,)),
            pltpu.SemaphoreType.DMA((2,)),
            pltpu.SemaphoreType.DMA((2,)),
            pltpu.SemaphoreType.DMA((2,)),
            pltpu.SemaphoreType.DMA((2,)),
        ],
        compiler_params=pltpu.CompilerParams(collective_id=0, has_side_effects=True),
        name="krum",
    )(winner, neighbours, gradients.reshape(length // LANES, LANES))
    return scores[0, :WORKERS], aggregate.reshape(-1)


def solution(mesh):
    split = Mesh(mesh.devices.reshape(4, 2, 2, 8, 2), AXES)
    in_specs = (P(WORKER, MP), P(), P())
    out_specs = (P(), P(MP_WORKER))
    return jax.shard_map(body, mesh=split, in_specs=in_specs, out_specs=out_specs, check_vma=False)
```

time: 112 us -> 40.9 us (0.37)
  the two profiles are of different devices: /device:TPU:6 before, /device:TPU:1 now
where the time goes in v1:
time: 40.9 us; the launch traced here: 40.7 us
  Pallas kernels  36.7 us (90%)
  local copies, waits for them, and re-layouts  2.74 us (7%)
  between operations  1.28 us (3%)
    pallas_call x1, Pallas kernels, body(): pl.pallas_call(functools.partial(kernel, total_entries), out_shape=(jax.S...  36.7 us
    unnamed x1, local copies, waits for them, and re-layouts  1.57 us
    squeeze x1, local copies, waits for them, and re-layouts, body(): return (scores[0, :WORKERS], aggregate.reshape(-1))  1.18 us

profile of v1, /device:TPU:1, one launch (start us, length us, event | category | flops | bytes accessed | tf_op | source)
XLA Modules:
  0.0 40.7 jit_solution(6071334495474262038)
XLA Ops:
  1.3 36.7 %krum.1 = (f32[1,128]{1,0:T(1,128)}, f32[256,128]{1,0:T(8,128)}) custom-call(s32[1]{0:T(128)S(6)} %copy.6.winner_ref, s32[16,11]{1,0:T(8,128)} %neighbours_ref.1, f32[4096,128]{1,0:T(8,128)} %bitcast.4), custom_call_target="tpu_custom_call" | custom-call | tf_op jit(solution)/shard_map/krum/pallas_call | solution.py:234
  38.0 1.2 %slice_bitcast_fusion = f32[16]{0:T(128)} fusion(f32[1,128]{1,0:T(1,128)} %get-tuple-element.4), kind=kLoop, calls=%fused_computation | loop fusion | bytes 128 | tf_op jit(solution)/shard_map/squeeze | solution.py:273
  39.2 1.6 %copy.7 = f32[32768]{0:T(1024)} copy(f32[32768]{0:T(1024)} %bitcast.5) | data formatting | bytes 262144

commit v2 on v1

--- a/solution.py
+++ b/solution.py
@@ -79,7 +79,7 @@
 def kernel(
     total_entries,
     winner_ref,
-    neighbours_ref,
+    neighbours_hbm,
     gradients_ref,
     scores_ref,
     aggregate_ref,
@@ -95,6 +95,7 @@
     line_got,
     plane_src,
     plane_got,
+    neighbours_ref,
     load_sem,
     hi_send,
     hi_recv,
@@ -106,8 +107,7 @@
     own_core = lax.axis_index("c")
     own_chip = chip_index((0, 0, 0, 0))
     own = worker_index((0, 0, 0, 0))
-    winner = winner_ref[0]
-
+    fetch = pltpu.make_async_copy(neighbours_hbm, neighbours_ref, load_sem.at[16])
     order = PEERS + [(0, 0, 0, 0)]
     loads = []
     for slot, offset in enumerate(order):
@@ -115,6 +115,7 @@
         load = pltpu.make_async_copy(gradients_ref.at[rows], full.at[slot], load_sem.at[slot])
         load.start()
         loads.append(load)
+    fetch.start()
 
     barrier = pltpu.get_barrier_semaphore()
     partners = LINE + PLANE
@@ -152,6 +153,8 @@
             )
     swap = send(lo_away, lo.at[own_core], lo_send.at[0], lo_recv.at[0], (0, 0, 0, 1))
 
+    fetch.wait()
+    winner = winner_ref[0]
     row = lax.broadcasted_iota(jnp.int32, (WORKERS, ROWS), 0)
     column = lax.broadcasted_iota(jnp.int32, (WORKERS, ROWS), 1) // 16
     counts = jnp.zeros((WORKERS, ROWS), jnp.float32)
@@ -227,6 +230,13 @@
     wait_bytes(plane_got, sum_send.at[1])
 
 
+def finish(row_ref, block_ref, scores_ref, aggregate_ref, sem):
+    copy = pltpu.make_async_copy(block_ref, aggregate_ref, sem)
+    copy.start()
+    scores_ref[...] = row_ref[0, :WORKERS]
+    copy.wait()
+
+
 def body(gradients, neighbours, winner):
     length = gradients.shape[1]
     total_entries = neighbours.shape[1] * length * lax.axis_size(MP)
@@ -239,8 +249,8 @@
         ),
         in_specs=[
             pl.BlockSpec(memory_space=pltpu.SMEM),
-            pl.BlockSpec(memory_space=pltpu.VMEM),
-            pl.BlockSpec(memory_space=pl.ANY),
+            pl.BlockSpec(memory_space=pltpu.HBM),
+            pl.BlockSpec(memory_space=pltpu.HBM),
         ],
         out_specs=(
             pl.BlockSpec(memory_space=pltpu.VMEM),
@@ -259,7 +269,8 @@
             pltpu.VMEM((len(LINE), 1, LANES), f32),
             pltpu.VMEM((1, LANES), f32),
             pltpu.VMEM((len(PLANE), 1, LANES), f32),
-            pltpu.SemaphoreType.DMA((16,)),
+            pltpu.VMEM(neighbours.shape, jnp.int32),
+            pltpu.SemaphoreType.DMA((17,)),
             pltpu.SemaphoreType.DMA((2,)),
             pltpu.SemaphoreType.DMA((2,)),
             pltpu.SemaphoreType.DMA((2,)),
@@ -267,10 +278,30 @@
             pltpu.SemaphoreType.DMA((2,)),
             pltpu.SemaphoreType.DMA((2,)),
         ],
-        compiler_params=pltpu.CompilerParams(collective_id=0, has_side_effects=True),
+        compiler_params=pltpu.CompilerParams(
+            collective_id=0, has_side_effects=True, vmem_limit_bytes=24 << 20
+        ),
         name="krum",
-    )(winner, neighbours, gradients.reshape(length // LANES, LANES))
-    return scores[0, :WORKERS], aggregate.reshape(-1)
+    )(
+        winner,
+        pltpu.with_memory_space_constraint(neighbours, pltpu.HBM),
+        pltpu.with_memory_space_constraint(
+            gradients.reshape(length // LANES, LANES), pltpu.HBM
+        ),
+    )
+    scores, aggregate = pl.pallas_call(
+        finish,
+        out_shape=(
+            jax.ShapeDtypeStruct((WORKERS,), f32),
+            jax.ShapeDtypeStruct((ROWS, LANES), f32),
+        ),
+        in_specs=[pl.BlockSpec(memory_space=pltpu.VMEM)] * 2,
+        out_specs=(pl.BlockSpec(memory_space=pltpu.VMEM), pl.BlockSpec(memory_space=pltpu.HBM)),
+        scratch_shapes=[pltpu.SemaphoreType.DMA],
+        compiler_params=pltpu.CompilerParams(vmem_limit_bytes=1 << 20),
+        name="finish",
+    )(scores, aggregate)
+    return scores, aggregate.reshape(-1)
 
 
 def solution(mesh):

time: 40.9 us -> 38 us (0.929)
  local copies, waits for them, and re-layouts: 2.74 us -> 0 us
    unnamed x1 -> x0, local copies, waits for them, and re-layouts: 1.57 us -> none
    pallas_call x1, Pallas kernels: 36.7 us -> 35.4 us  [body(): pl.pallas_call(functools.partial(kernel, total_entries), out_shape=(jax.S...]
    squeeze x1 -> x0, local copies, waits for them, and re-layouts: 1.18 us -> none  [body(): return (scores[0, :WORKERS], aggregate.reshape(-1))]
    pallas_call x0 -> x1, Pallas kernels: none -> 1.17 us  [body(): pl.pallas_call(finish, out_shape=(jax.ShapeDtypeStruct((WORKERS,), f32),...]
where the time goes in v2:
time: 38 us; the launch traced here: 37.9 us
  Pallas kernels  36.6 us (96%)
  between operations  1.28 us (3%)
    pallas_call x1, Pallas kernels, body(): pl.pallas_call(functools.partial(kernel, total_entries), out_shape=(jax.S...  35.4 us
    pallas_call x1, Pallas kernels, body(): pl.pallas_call(finish, out_shape=(jax.ShapeDtypeStruct((WORKERS,), f32),...  1.17 us

profile of v2, /device:TPU:1, one launch (start us, length us, event | category | flops | bytes accessed | tf_op | source)
XLA Modules:
  0.0 37.9 jit_solution(16053269855815871044)
XLA Ops:
  1.3 35.4 %krum.1 = (f32[1,128]{1,0:T(1,128)S(1)}, f32[256,128]{1,0:T(8,128)S(1)}) custom-call(s32[1]{0:T(128)S(6)} %copy.5.winner_ref, s32[16,11]{1,0:T(8,128)} %neighbours_hbm.1, f32[4096,128]{1,0:T(8,128)} %bitcast.2), custom_call_target="tpu_custom_call" | custom-call | tf_op jit(solution)/shard_map/krum/pallas_call | solution.py:244
  36.7 1.2 %finish.1 = (f32[16]{0:T(128)}, f32[256,128]{1,0:T(8,128)}) custom-call(f32[1,128]{1,0:T(1,128)S(1)} %get-tuple-element.6.row_ref, f32[256,128]{1,0:T(8,128)S(1)} %get-tuple-element.7.block_ref), custom_call_target="tpu_custom_call" | custom-call | tf_op jit(solution)/shard_map/finish/pallas_call | solution.py:292

commit v3 on v2

v3 whole, which is shorter than its diff:
```python
import functools

import jax
import jax.numpy as jnp
from jax import lax
from jax.experimental import pallas as pl
from jax.experimental.pallas import tpu as pltpu
from jax.sharding import Mesh
from jax.sharding import PartitionSpec as P

AXES = ("y", "xh", "c", "z", "xl")
WORKER = ("y", "xh", "c")
MP = ("z", "xl")
MP_WORKER = ("z", "xl", "y", "xh", "c")
MESH = pl.DeviceIdType.MESH

WORKERS = 16
ROWS = 256
LANES = 128

PAIR = (0, 0, 0, 1)
ACROSS = (2, 0, 0, 0)
PASSED = [(2, dy, 0, dc) for dy in (2, 1, 3) for dc in (0, 1)]
DIRECT = [(2, 0, 0, 1), ACROSS]
COLUMN = [(0, dy, 0, dc) for dy in (2, 1, 3) for dc in (0, 1)] + [PAIR]
CHIPS = [(2, 2), (2, 0), (0, 2), (2, 1), (0, 1), (2, 3), (0, 3)]
SIDES = [(1, 0, 0, 0), (3, 0, 0, 0)]
ENDS = [(0, 0, 1, 0), (0, 0, 7, 0)]
ROUNDS = 4
SLICE = [
    (dx, dy, dz, 0)
    for dx, dy, dz in sorted(
        ((a, b, d) for a in range(4) for b in range(4) for d in range(8)),
        key=lambda p: -(min(p[0], 4 - p[0]) + min(p[1], 4 - p[1]) + min(p[2], 8 - p[2])),
    )
    if (dx, dy, dz) != (0, 0, 0)
]


class Place:
    def __init__(self):
        x = lax.axis_index("xh") * 2 + lax.axis_index("xl")
        own = (x, lax.axis_index("y"), lax.axis_index("z"), lax.axis_index("c"))
        self.steps = [
            [value] + [lax.rem(value + step, size) for step in range(1, size)]
            for value, size in zip(own, (4, 4, 8, 2))
        ]
        self.x_hi = [x // 2 for x in self.steps[0]]
        self.x_lo = [lax.rem(x, 2) for x in self.steps[0]]

    def device(self, offset):
        dx, dy, dz, dc = offset
        _, y, z, c = self.steps
        return {"y": y[dy], "xh": self.x_hi[dx], "c": c[dc], "z": z[dz], "xl": self.x_lo[dx]}

    def chip(self, offset):
        return self.steps[1][offset[1]] * 2 + self.x_hi[offset[0]]

    def worker(self, offset):
        return self.chip(offset) * 2 + self.steps[3][offset[3]]

    def signal(self, sem, offset):
        pl.semaphore_signal(sem, inc=1, device_id=self.device(offset), device_id_type=MESH)

    def send(self, src, dst, send_sem, recv_sem, offset):
        pltpu.make_async_remote_copy(
            src_ref=src,
            dst_ref=dst,
            send_sem=send_sem,
            recv_sem=recv_sem,
            device_id=self.device(offset),
            device_id_type=MESH,
        ).start()


def wait_bytes(ref, sem):
    pltpu.make_async_copy(ref, ref, sem).wait()


def kernel(
    total_entries,
    winner_ref,
    neighbours_hbm,
    gradients_ref,
    scores_ref,
    aggregate_ref,
    full,
    hi,
    passing,
    got,
    lo,
    lo_away,
    lo_mine,
    lo_got,
    own_sum,
    pair_got,
    pair_sum,
    sums_got,
    neighbours_ref,
    load_sem,
    hi_send,
    hi_recv,
    pass_recv,
    lo_send,
    lo_recv,
    sum_send,
    sum_recv,
    plane_in,
    line_in,
):
    here = Place()
    home = (0, 0, 0, 0)
    own_core = here.steps[3][0]
    own_chip = here.chip(home)
    own = here.worker(home)

    order = PASSED + COLUMN + DIRECT + [home]
    loads = []
    for slot, offset in enumerate(order):
        rows = pl.ds(pl.multiple_of(here.worker(offset) * ROWS, ROWS), ROWS)
        load = pltpu.make_async_copy(gradients_ref.at[rows], full.at[slot], load_sem.at[slot])
        load.start()
        loads.append(load)
    fetch = pltpu.make_async_copy(neighbours_hbm, neighbours_ref, load_sem.at[WORKERS])
    fetch.start()

    barrier = pltpu.get_barrier_semaphore()
    partners = COLUMN + DIRECT + SIDES + ENDS
    for offset in partners:
        here.signal(barrier, offset)

    for slot, offset in enumerate(order):
        loads[slot].wait()
        value = full[slot]
        high = value.astype(jnp.bfloat16)
        low = (value - high.astype(jnp.float32)).astype(jnp.bfloat16)
        if offset == home:
            got[own] = high
        else:
            hi[slot] = high
        if offset[3] == 0:
            lo[own_core, here.chip(offset)] = low
        else:
            lo_away[here.chip(offset)] = low

    pl.semaphore_wait(barrier, len(partners))

    for slot, offset in enumerate(order):
        if offset in PASSED:
            here.send(hi.at[slot], passing.at[slot], hi_send, pass_recv.at[slot], ACROSS)
    for slot, offset in enumerate(order):
        if offset in COLUMN + DIRECT:
            here.send(hi.at[slot], got.at[own], hi_send, hi_recv, offset)
    for offset in SIDES + [ACROSS]:
        here.signal(plane_in, offset)
    here.send(lo_away, lo.at[own_core], lo_send.at[0], lo_recv.at[0], PAIR)

    fetch.wait()
    winner = winner_ref[0]
    row = lax.broadcasted_iota(jnp.int32, (WORKERS, ROWS), 0)
    column = lax.broadcasted_iota(jnp.int32, (WORKERS, ROWS), 1) // 16
    counts = jnp.zeros((WORKERS, ROWS), jnp.float32)
    for entry in range(neighbours_ref.shape[1]):
        counts += (neighbours_ref[:, entry : entry + 1] == column).astype(jnp.float32)
    own_sum[...] = jnp.zeros_like(own_sum)

    wait_bytes(lo_away, lo_recv.at[0])
    lo_mine[...] = lo[lax.rem(winner, 2)]

    pl.semaphore_wait(plane_in, len(SIDES) + 1)
    across = here.worker(ACROSS)
    for slot, (_, dy, _, dc) in enumerate(PASSED):
        if slot < ROUNDS:
            for offset in ENDS:
                here.signal(line_in.at[slot], offset)
        wait_bytes(passing.at[slot], pass_recv.at[slot])
        here.send(passing.at[slot], got.at[across], hi_send, hi_recv, (0, dy, 0, dc))
        if slot < ROUNDS:
            pl.semaphore_wait(line_in.at[slot], len(ENDS))

    wait_bytes(got.at[pl.ds(0, 15)], hi_recv)
    for dx, dy in CHIPS:
        offset = (dx, dy, 0, 0)
        here.send(
            lo_mine.at[here.chip(offset)],
            lo_got.at[own_chip],
            lo_send.at[1],
            lo_recv.at[1],
            offset,
        )
    lo_got[own_chip] = lo_mine[own_chip]

    parts = [got[:, pl.ds(step * 16, 16), :].reshape(ROWS, LANES) for step in range(ROWS // 16)]
    block = jnp.concatenate(parts, axis=1)
    total = lax.dot_general(
        block, block, (((1,), (1,)), ((), ())), preferred_element_type=jnp.float32
    )
    sublane = lax.broadcasted_iota(jnp.int32, (ROWS, ROWS), 0)
    lane = lax.broadcasted_iota(jnp.int32, (ROWS, ROWS), 1)
    total = jnp.where(lax.rem(sublane, 16) == lax.rem(lane, 16), total, 0.0)
    total = jnp.sum(total.reshape(WORKERS, 16, ROWS), axis=1)
    diagonal = jnp.where(row == column, total, 0.0)
    squares = jnp.sum(diagonal, axis=0, keepdims=True)
    own_counts = jnp.sum(counts, axis=1, keepdims=True) * (1.0 / 16.0)
    partial = counts * (squares - 2.0 * total) + own_counts * diagonal
    partial = lax.dot_general(
        jnp.ones((8, ROWS), jnp.float32),
        partial,
        (((1,), (1,)), ((), ())),
        precision=lax.Precision.HIGHEST,
        preferred_element_type=jnp.float32,
    )
    own_sum[:, pl.ds(0, WORKERS)] = partial[0:1]

    here.send(own_sum, pair_got, sum_send.at[0], sum_recv.at[0], PAIR)
    wait_bytes(pair_got, sum_recv.at[0])
    pair_sum[...] = own_sum[...] + pair_got[...]
    for step, offset in enumerate(SLICE):
        here.send(pair_sum, sums_got.at[step], sum_send.at[1], sum_recv.at[1], offset)

    wait_bytes(lo_got.at[pl.ds(0, 7)], lo_recv.at[1])
    aggregate_ref[...] = got[winner].astype(jnp.float32) + lo_got[winner // 2].astype(jnp.float32)

    wait_bytes(sums_got, sum_recv.at[1])
    scores = pair_sum[...] + jnp.sum(sums_got[...], axis=0)
    scores_ref[...] = scores / jnp.float32(total_entries)

    wait_bytes(got.at[pl.ds(0, 15)], hi_send)
    wait_bytes(passing, hi_send)
    wait_bytes(lo_away, lo_send.at[0])
    wait_bytes(lo_got.at[pl.ds(0, 7)], lo_send.at[1])
    wait_bytes(pair_got, sum_send.at[0])
    wait_bytes(sums_got, sum_send.at[1])


def finish(row_ref, block_ref, scores_ref, aggregate_ref, sem):
    copy = pltpu.make_async_copy(block_ref, aggregate_ref, sem)
    copy.start()
    scores_ref[...] = row_ref[0, :WORKERS]
    copy.wait()


def body(gradients, neighbours, winner):
    length = gradients.shape[1]
    total_entries = neighbours.shape[1] * length * lax.axis_size(MP)
    bf16, f32 = jnp.bfloat16, jnp.float32
    out_shape = (
        jax.ShapeDtypeStruct((1, LANES), f32),
        jax.ShapeDtypeStruct((ROWS, LANES), f32),
    )
    scores, aggregate = pl.pallas_call(
        functools.partial(kernel, total_entries),
        out_shape=out_shape,
        in_specs=[
            pl.BlockSpec(memory_space=pltpu.SMEM),
            pl.BlockSpec(memory_space=pltpu.HBM),
            pl.BlockSpec(memory_space=pltpu.HBM),
        ],
        out_specs=(pl.BlockSpec(memory_space=pltpu.VMEM),) * 2,
        scratch_shapes=[
            pltpu.VMEM((WORKERS, ROWS, LANES), f32),
            pltpu.VMEM((15, ROWS, LANES), bf16),
            pltpu.VMEM((len(PASSED), ROWS, LANES), bf16),
            pltpu.VMEM((WORKERS, ROWS, LANES), bf16),
            pltpu.VMEM((2, 8, ROWS, LANES), bf16),
            pltpu.VMEM((8, ROWS, LANES), bf16),
            pltpu.VMEM((8, ROWS, LANES), bf16),
            pltpu.VMEM((8, ROWS, LANES), bf16),
            pltpu.VMEM((1, LANES), f32),
            pltpu.VMEM((1, LANES), f32),
            pltpu.VMEM((1, LANES), f32),
            pltpu.VMEM((len(SLICE), 1, LANES), f32),
            pltpu.VMEM(neighbours.shape, jnp.int32),
            pltpu.SemaphoreType.DMA((WORKERS + 1,)),
            pltpu.SemaphoreType.DMA,
            pltpu.SemaphoreType.DMA,
            pltpu.SemaphoreType.DMA((len(PASSED),)),
            pltpu.SemaphoreType.DMA((2,)),
            pltpu.SemaphoreType.DMA((2,)),
            pltpu.SemaphoreType.DMA((2,)),
            pltpu.SemaphoreType.DMA((2,)),
            pltpu.SemaphoreType.REGULAR,
            pltpu.SemaphoreType.REGULAR((ROUNDS,)),
        ],
        compiler_params=pltpu.CompilerParams(
            collective_id=0, has_side_effects=True, vmem_limit_bytes=24 << 20
        ),
        name="krum",
    )(
        winner,
        pltpu.with_memory_space_constraint(neighbours, pltpu.HBM),
        pltpu.with_memory_space_constraint(
            gradients.reshape(length // LANES, LANES), pltpu.HBM
        ),
    )
    scores, aggregate = pl.pallas_call(
        finish,
        out_shape=(jax.ShapeDtypeStruct((WORKERS,), f32), out_shape[1]),
        in_specs=[pl.BlockSpec(memory_space=pltpu.VMEM)] * 2,
        out_specs=(pl.BlockSpec(memory_space=pltpu.VMEM), pl.BlockSpec(memory_space=pltpu.HBM)),
        scratch_shapes=[pltpu.SemaphoreType.DMA],
        compiler_params=pltpu.CompilerParams(vmem_limit_bytes=1 << 20),
        name="finish",
    )(scores, aggregate)
    return scores, aggregate.reshape(-1)


def solution(mesh):
    split = Mesh(mesh.devices.reshape(4, 2, 2, 8, 2), AXES)
    in_specs = (P(WORKER, MP), P(), P())
    out_specs = (P(), P(MP_WORKER))
    return jax.shard_map(body, mesh=split, in_specs=in_specs, out_specs=out_specs, check_vma=False)
```

time: 38 us -> 36.6 us (0.963)
  Pallas kernels: 36.6 us -> 35.2 us
    pallas_call x1, Pallas kernels: 35.4 us -> 34 us  [body(): pl.pallas_call(functools.partial(kernel, total_entries), out_shape=out_sh...]
where the time goes in v3:
time: 36.6 us; the launch traced here: 36.5 us
  Pallas kernels  35.2 us (96%)
  between operations  1.28 us (3%)
    pallas_call x1, Pallas kernels, body(): pl.pallas_call(functools.partial(kernel, total_entries), out_shape=out_sh...  34 us
    pallas_call x1, Pallas kernels, body(): pl.pallas_call(finish, out_shape=(jax.ShapeDtypeStruct((WORKERS,), f32),...  1.17 us

profile of v3, /device:TPU:1, one launch (start us, length us, event | category | flops | bytes accessed | tf_op | source)
XLA Modules:
  0.0 36.5 jit_solution(8042197585578559970)
XLA Ops:
  1.3 34.0 %krum.1 = (f32[1,128]{1,0:T(1,128)S(1)}, f32[256,128]{1,0:T(8,128)S(1)}) custom-call(s32[1]{0:T(128)S(6)} %copy.5.winner_ref, s32[16,11]{1,0:T(8,128)} %neighbours_hbm.1, f32[4096,128]{1,0:T(8,128)} %bitcast.2), custom_call_target="tpu_custom_call" | custom-call | tf_op jit(solution)/shard_map/krum/pallas_call | solution.py:251
  35.3 1.2 %finish.1 = (f32[16]{0:T(128)}, f32[256,128]{1,0:T(8,128)}) custom-call(f32[1,128]{1,0:T(1,128)S(1)} %get-tuple-element.6.row_ref, f32[256,128]{1,0:T(8,128)S(1)} %get-tuple-element.7.block_ref), custom_call_target="tpu_custom_call" | custom-call | tf_op jit(solution)/shard_map/finish/pallas_call | solution.py:296

commit v4 on v3

--- a/solution.py
+++ b/solution.py
@@ -20,10 +20,11 @@
 
 PAIR = (0, 0, 0, 1)
 ACROSS = (2, 0, 0, 0)
-PASSED = [(2, dy, 0, dc) for dy in (2, 1, 3) for dc in (0, 1)]
+PASSED = [(2, dy, 0, dc) for dy, dc in ((2, 0), (2, 1), (1, 0), (3, 0), (1, 1), (3, 1))]
 DIRECT = [(2, 0, 0, 1), ACROSS]
 COLUMN = [(0, dy, 0, dc) for dy in (2, 1, 3) for dc in (0, 1)] + [PAIR]
-CHIPS = [(2, 2), (2, 0), (0, 2), (2, 1), (0, 1), (2, 3), (0, 3)]
+LOW_ACROSS = [(2, dy, 0, 0) for dy in (2, 1, 3, 0)]
+LOW_COLUMN = [(0, dy, 0, 0) for dy in (2, 1, 3)]
 SIDES = [(1, 0, 0, 0), (3, 0, 0, 0)]
 ENDS = [(0, 0, 1, 0), (0, 0, 7, 0)]
 ROUNDS = 4
@@ -129,6 +130,13 @@
     for offset in partners:
         here.signal(barrier, offset)
 
+    def start(slot):
+        offset = order[slot]
+        if offset in PASSED:
+            here.send(hi.at[slot], passing.at[slot], hi_send, pass_recv.at[slot], ACROSS)
+        elif offset != home:
+            here.send(hi.at[slot], got.at[own], hi_send, hi_recv, offset)
+
     for slot, offset in enumerate(order):
         loads[slot].wait()
         value = full[slot]
@@ -142,15 +150,13 @@
             lo[own_core, here.chip(offset)] = low
         else:
             lo_away[here.chip(offset)] = low
-
-    pl.semaphore_wait(barrier, len(partners))
-
-    for slot, offset in enumerate(order):
-        if offset in PASSED:
-            here.send(hi.at[slot], passing.at[slot], hi_send, pass_recv.at[slot], ACROSS)
-    for slot, offset in enumerate(order):
-        if offset in COLUMN + DIRECT:
-            here.send(hi.at[slot], got.at[own], hi_send, hi_recv, offset)
+        if slot == 1:
+            pl.semaphore_wait(barrier, len(partners))
+            for ready in range(1 + 1):
+                start(ready)
+        if slot > 1:
+            start(slot)
+
     for offset in SIDES + [ACROSS]:
         here.signal(plane_in, offset)
     here.send(lo_away, lo.at[own_core], lo_send.at[0], lo_recv.at[0], PAIR)
@@ -179,8 +185,9 @@
             pl.semaphore_wait(line_in.at[slot], len(ENDS))
 
     wait_bytes(got.at[pl.ds(0, 15)], hi_recv)
-    for dx, dy in CHIPS:
-        offset = (dx, dy, 0, 0)
+    lo_got[own_chip] = lo_mine[own_chip]
+
+    for offset in LOW_ACROSS + LOW_COLUMN:
         here.send(
             lo_mine.at[here.chip(offset)],
             lo_got.at[own_chip],
@@ -188,8 +195,6 @@
             lo_recv.at[1],
             offset,
         )
-    lo_got[own_chip] = lo_mine[own_chip]
-
     parts = [got[:, pl.ds(step * 16, 16), :].reshape(ROWS, LANES) for step in range(ROWS // 16)]
     block = jnp.concatenate(parts, axis=1)
     total = lax.dot_general(

time: 36.6 us -> 35.9 us (0.981)
  Pallas kernels: 35.2 us -> 34.5 us
    pallas_call x1, Pallas kernels: 34 us -> 33.3 us  [body(): pl.pallas_call(functools.partial(kernel, total_entries), out_shape=out_sh...]
where the time goes in v4:
time: 35.9 us; the launch traced here: 35.8 us
  Pallas kernels  34.5 us (96%)
  between operations  1.28 us (4%)
    pallas_call x1, Pallas kernels, body(): pl.pallas_call(functools.partial(kernel, total_entries), out_shape=out_sh...  33.3 us
    pallas_call x1, Pallas kernels, body(): pl.pallas_call(finish, out_shape=(jax.ShapeDtypeStruct((WORKERS,), f32),...  1.17 us

profile of v4, /device:TPU:1, one launch (start us, length us, event | category | flops | bytes accessed | tf_op | source)
XLA Modules:
  0.0 35.8 jit_solution(6736411969842791828)
XLA Ops:
  1.3 33.3 %krum.1 = (f32[1,128]{1,0:T(1,128)S(1)}, f32[256,128]{1,0:T(8,128)S(1)}) custom-call(s32[1]{0:T(128)S(6)} %copy.5.winner_ref, s32[16,11]{1,0:T(8,128)} %neighbours_hbm.1, f32[4096,128]{1,0:T(8,128)} %bitcast.2), custom_call_target="tpu_custom_call" | custom-call | tf_op jit(solution)/shard_map/krum/pallas_call | solution.py:256
  34.6 1.2 %finish.1 = (f32[16]{0:T(128)}, f32[256,128]{1,0:T(8,128)}) custom-call(f32[1,128]{1,0:T(1,128)S(1)} %get-tuple-element.6.row_ref, f32[256,128]{1,0:T(8,128)S(1)} %get-tuple-element.7.block_ref), custom_call_target="tpu_custom_call" | custom-call | tf_op jit(solution)/shard_map/finish/pallas_call | solution.py:301

commit v5 on v4

--- a/solution.py
+++ b/solution.py
@@ -20,7 +20,8 @@
 
 PAIR = (0, 0, 0, 1)
 ACROSS = (2, 0, 0, 0)
-PASSED = [(2, dy, 0, dc) for dy, dc in ((2, 0), (2, 1), (1, 0), (3, 0), (1, 1), (3, 1))]
+PASSED = [(2, dy, 0, dc) for dy, dc in ((2, 0), (2, 1),)]
+LATE = [(2, dy, 0, dc) for dy, dc in ((1, 0), (3, 0), (1, 1), (3, 1),)]
 DIRECT = [(2, 0, 0, 1), ACROSS]
 COLUMN = [(0, dy, 0, dc) for dy in (2, 1, 3) for dc in (0, 1)] + [PAIR]
 LOW_ACROSS = [(2, dy, 0, 0) for dy in (2, 1, 3, 0)]
@@ -115,7 +116,12 @@
     own_chip = here.chip(home)
     own = here.worker(home)
 
-    order = PASSED + COLUMN + DIRECT + [home]
+    barrier = pltpu.get_barrier_semaphore()
+    partners = COLUMN + DIRECT + SIDES + ENDS
+    for offset in partners:
+        here.signal(barrier, offset)
+
+    order = PASSED + COLUMN + DIRECT + LATE + [home]
     loads = []
     for slot, offset in enumerate(order):
         rows = pl.ds(pl.multiple_of(here.worker(offset) * ROWS, ROWS), ROWS)
@@ -125,16 +131,11 @@
     fetch = pltpu.make_async_copy(neighbours_hbm, neighbours_ref, load_sem.at[WORKERS])
     fetch.start()
 
-    barrier = pltpu.get_barrier_semaphore()
-    partners = COLUMN + DIRECT + SIDES + ENDS
-    for offset in partners:
-        here.signal(barrier, offset)
-
     def start(slot):
         offset = order[slot]
         if offset in PASSED:
             here.send(hi.at[slot], passing.at[slot], hi_send, pass_recv.at[slot], ACROSS)
-        elif offset != home:
+        elif offset != home and offset not in LATE:
             here.send(hi.at[slot], got.at[own], hi_send, hi_recv, offset)
 
     for slot, offset in enumerate(order):
@@ -174,13 +175,18 @@
     lo_mine[...] = lo[lax.rem(winner, 2)]
 
     pl.semaphore_wait(plane_in, len(SIDES) + 1)
+    for slot, offset in enumerate(order):
+        if offset in LATE:
+            here.send(hi.at[slot], got.at[own], hi_send, hi_recv, offset)
     across = here.worker(ACROSS)
-    for slot, (_, dy, _, dc) in enumerate(PASSED):
+    for slot in range(max(ROUNDS, len(PASSED))):
         if slot < ROUNDS:
             for offset in ENDS:
                 here.signal(line_in.at[slot], offset)
-        wait_bytes(passing.at[slot], pass_recv.at[slot])
-        here.send(passing.at[slot], got.at[across], hi_send, hi_recv, (0, dy, 0, dc))
+        if slot < len(PASSED):
+            _, dy, _, dc = PASSED[slot]
+            wait_bytes(passing.at[slot], pass_recv.at[slot])
+            here.send(passing.at[slot], got.at[across], hi_send, hi_recv, (0, dy, 0, dc))
         if slot < ROUNDS:
             pl.semaphore_wait(line_in.at[slot], len(ENDS))
 
@@ -228,7 +234,7 @@
 
     wait_bytes(sums_got, sum_recv.at[1])
     scores = pair_sum[...] + jnp.sum(sums_got[...], axis=0)
-    scores_ref[...] = scores / jnp.float32(total_entries)
+    scores_ref[...] = scores[0, :WORKERS] / jnp.float32(total_entries)
 
     wait_bytes(got.at[pl.ds(0, 15)], hi_send)
     wait_bytes(passing, hi_send)
@@ -238,11 +244,15 @@
     wait_bytes(sums_got, sum_send.at[1])
 
 
-def finish(row_ref, block_ref, scores_ref, aggregate_ref, sem):
-    copy = pltpu.make_async_copy(block_ref, aggregate_ref, sem)
-    copy.start()
-    scores_ref[...] = row_ref[0, :WORKERS]
-    copy.wait()
+def finish(scores_ref, block_ref, scores_hbm, block_hbm, sem):
+    copies = (
+        pltpu.make_async_copy(scores_ref, scores_hbm, sem.at[0]),
+        pltpu.make_async_copy(block_ref, block_hbm, sem.at[1]),
+    )
+    for copy in copies:
+        copy.start()
+    for copy in copies:
+        copy.wait()
 
 
 def body(gradients, neighbours, winner):
@@ -250,7 +260,7 @@
     total_entries = neighbours.shape[1] * length * lax.axis_size(MP)
     bf16, f32 = jnp.bfloat16, jnp.float32
     out_shape = (
-        jax.ShapeDtypeStruct((1, LANES), f32),
+        jax.ShapeDtypeStruct((WORKERS,), f32),
         jax.ShapeDtypeStruct((ROWS, LANES), f32),
     )
     scores, aggregate = pl.pallas_call(
@@ -300,10 +310,10 @@
     )
     scores, aggregate = pl.pallas_call(
         finish,
-        out_shape=(jax.ShapeDtypeStruct((WORKERS,), f32), out_shape[1]),
+        out_shape=out_shape,
         in_specs=[pl.BlockSpec(memory_space=pltpu.VMEM)] * 2,
-        out_specs=(pl.BlockSpec(memory_space=pltpu.VMEM), pl.BlockSpec(memory_space=pltpu.HBM)),
-        scratch_shapes=[pltpu.SemaphoreType.DMA],
+        out_specs=(pl.BlockSpec(memory_space=pltpu.HBM),) * 2,
+        scratch_shapes=[pltpu.SemaphoreType.DMA((2,))],
         compiler_params=pltpu.CompilerParams(vmem_limit_bytes=1 << 20),
         name="finish",
     )(scores, aggregate)

time: 35.9 us -> 34.7 us (0.967)
  Pallas kernels: 34.5 us -> 33.4 us
    pallas_call x1, Pallas kernels: 33.3 us -> 32.7 us  [body(): pl.pallas_call(functools.partial(kernel, total_entries), out_shape=out_sh...]
    pallas_call x1, Pallas kernels: 1.17 us -> 0.68 us  [body(): pl.pallas_call(finish, out_shape=out_shape, in_specs=[pl.BlockSpec(memory...]
where the time goes in v5:
time: 34.7 us; the launch traced here: 34.6 us
  Pallas kernels  33.4 us (96%)
  between operations  1.28 us (4%)
    pallas_call x1, Pallas kernels, body(): pl.pallas_call(functools.partial(kernel, total_entries), out_shape=out_sh...  32.7 us

profile of v5, /device:TPU:1, one launch (start us, length us, event | category | flops | bytes accessed | tf_op | source)
XLA Modules:
  0.0 34.6 jit_solution(13157636781539676828)
XLA Ops:
  1.3 32.7 %krum.1 = (f32[16]{0:T(128)S(1)}, f32[256,128]{1,0:T(8,128)S(1)}) custom-call(s32[1]{0:T(128)S(6)} %copy.5.winner_ref, s32[16,11]{1,0:T(8,128)} %neighbours_hbm.1, f32[4096,128]{1,0:T(8,128)} %bitcast.2), custom_call_target="tpu_custom_call" | custom-call | tf_op jit(solution)/shard_map/krum/pallas_call | solution.py:266
  34.0 0.7 %finish.1 = (f32[16]{0:T(128)}, f32[256,128]{1,0:T(8,128)}) custom-call(f32[16]{0:T(128)S(1)} %get-tuple-element.6.scores_ref, f32[256,128]{1,0:T(8,128)S(1)} %get-tuple-element.7.block_ref), custom_call_target="tpu_custom_call" | custom-call | tf_op jit(solution)/shard_map/finish/pallas_call | solution.py:311

commit v6 on v5

--- a/solution.py
+++ b/solution.py
@@ -101,6 +101,7 @@
     neighbours_ref,
     load_sem,
     hi_send,
+    over_send,
     hi_recv,
     pass_recv,
     lo_send,
@@ -134,8 +135,10 @@
     def start(slot):
         offset = order[slot]
         if offset in PASSED:
-            here.send(hi.at[slot], passing.at[slot], hi_send, pass_recv.at[slot], ACROSS)
-        elif offset != home and offset not in LATE:
+            here.send(hi.at[slot], passing.at[slot], over_send, pass_recv.at[slot], ACROSS)
+        elif offset in DIRECT:
+            here.send(hi.at[slot], got.at[own], over_send, hi_recv, offset)
+        elif offset in COLUMN:
             here.send(hi.at[slot], got.at[own], hi_send, hi_recv, offset)
 
     for slot, offset in enumerate(order):
@@ -169,7 +172,6 @@
     counts = jnp.zeros((WORKERS, ROWS), jnp.float32)
     for entry in range(neighbours_ref.shape[1]):
         counts += (neighbours_ref[:, entry : entry + 1] == column).astype(jnp.float32)
-    own_sum[...] = jnp.zeros_like(own_sum)
 
     wait_bytes(lo_away, lo_recv.at[0])
     lo_mine[...] = lo[lax.rem(winner, 2)]
@@ -177,7 +179,7 @@
     pl.semaphore_wait(plane_in, len(SIDES) + 1)
     for slot, offset in enumerate(order):
         if offset in LATE:
-            here.send(hi.at[slot], got.at[own], hi_send, hi_recv, offset)
+            here.send(hi.at[slot], got.at[own], over_send, hi_recv, offset)
     across = here.worker(ACROSS)
     for slot in range(max(ROUNDS, len(PASSED))):
         if slot < ROUNDS:
@@ -190,10 +192,19 @@
         if slot < ROUNDS:
             pl.semaphore_wait(line_in.at[slot], len(ENDS))
 
+    wait_bytes(hi.at[pl.ds(0, 8)], over_send)
+    for offset in LOW_ACROSS:
+        here.send(
+            lo_mine.at[here.chip(offset)],
+            lo_got.at[own_chip],
+            lo_send.at[1],
+            lo_recv.at[1],
+            offset,
+        )
     wait_bytes(got.at[pl.ds(0, 15)], hi_recv)
     lo_got[own_chip] = lo_mine[own_chip]
 
-    for offset in LOW_ACROSS + LOW_COLUMN:
+    for offset in LOW_COLUMN:
         here.send(
             lo_mine.at[here.chip(offset)],
             lo_got.at[own_chip],
@@ -214,14 +225,10 @@
     squares = jnp.sum(diagonal, axis=0, keepdims=True)
     own_counts = jnp.sum(counts, axis=1, keepdims=True) * (1.0 / 16.0)
     partial = counts * (squares - 2.0 * total) + own_counts * diagonal
-    partial = lax.dot_general(
-        jnp.ones((8, ROWS), jnp.float32),
-        partial,
-        (((1,), (1,)), ((), ())),
-        precision=lax.Precision.HIGHEST,
-        preferred_element_type=jnp.float32,
-    )
-    own_sum[:, pl.ds(0, WORKERS)] = partial[0:1]
+    partial = jnp.sum(partial, axis=1, keepdims=True)
+    place = lax.broadcasted_iota(jnp.int32, (WORKERS, LANES), 1)
+    partial = jnp.where(row[:, :LANES] == place, partial, 0.0)
+    own_sum[...] = jnp.sum(partial, axis=0, keepdims=True)
 
     here.send(own_sum, pair_got, sum_send.at[0], sum_recv.at[0], PAIR)
     wait_bytes(pair_got, sum_recv.at[0])
@@ -236,8 +243,7 @@
     scores = pair_sum[...] + jnp.sum(sums_got[...], axis=0)
     scores_ref[...] = scores[0, :WORKERS] / jnp.float32(total_entries)
 
-    wait_bytes(got.at[pl.ds(0, 15)], hi_send)
-    wait_bytes(passing, hi_send)
+    wait_bytes(got.at[pl.ds(0, len(COLUMN) + len(PASSED))], hi_send)
     wait_bytes(lo_away, lo_send.at[0])
     wait_bytes(lo_got.at[pl.ds(0, 7)], lo_send.at[1])
     wait_bytes(pair_got, sum_send.at[0])
@@ -289,6 +295,7 @@
             pltpu.SemaphoreType.DMA((WORKERS + 1,)),
             pltpu.SemaphoreType.DMA,
             pltpu.SemaphoreType.DMA,
+            pltpu.SemaphoreType.DMA,
             pltpu.SemaphoreType.DMA((len(PASSED),)),
             pltpu.SemaphoreType.DMA((2,)),
             pltpu.SemaphoreType.DMA((2,)),

time: 34.7 us -> 34.4 us (level)
  Pallas kernels: 33.4 us -> 33 us
    pallas_call x1, Pallas kernels: 32.7 us -> 32.3 us  [body(): pl.pallas_call(functools.partial(kernel, total_entries), out_shape=out_sh...]
where the time goes in v6:
time: 34.4 us; the launch traced here: 34.3 us
  Pallas kernels  33 us (96%)
  between operations  1.28 us (4%)
    pallas_call x1, Pallas kernels, body(): pl.pallas_call(functools.partial(kernel, total_entries), out_shape=out_sh...  32.3 us

profile of v6, /device:TPU:1, one launch (start us, length us, event | category | flops | bytes accessed | tf_op | source)
XLA Modules:
  0.0 34.3 jit_solution(2443357191290321441)
XLA Ops:
  1.3 32.3 %krum.1 = (f32[16]{0:T(128)S(1)}, f32[256,128]{1,0:T(8,128)S(1)}) custom-call(s32[1]{0:T(128)S(6)} %copy.5.winner_ref, s32[16,11]{1,0:T(8,128)} %neighbours_hbm.1, f32[4096,128]{1,0:T(8,128)} %bitcast.2), custom_call_target="tpu_custom_call" | custom-call | tf_op jit(solution)/shard_map/krum/pallas_call | solution.py:272
  33.6 0.7 %finish.1 = (f32[16]{0:T(128)}, f32[256,128]{1,0:T(8,128)}) custom-call(f32[16]{0:T(128)S(1)} %get-tuple-element.6.scores_ref, f32[256,128]{1,0:T(8,128)S(1)} %get-tuple-element.7.block_ref), custom_call_target="tpu_custom_call" | custom-call | tf_op jit(solution)/shard_map/finish/pallas_call | solution.py:318

commit v7 on v6

--- a/solution.py
+++ b/solution.py
@@ -29,6 +29,7 @@
 SIDES = [(1, 0, 0, 0), (3, 0, 0, 0)]
 ENDS = [(0, 0, 1, 0), (0, 0, 7, 0)]
 ROUNDS = 4
+BEFORE = 2
 SLICE = [
     (dx, dy, dz, 0)
     for dx, dy, dz in sorted(
@@ -154,12 +155,12 @@
             lo[own_core, here.chip(offset)] = low
         else:
             lo_away[here.chip(offset)] = low
-        if slot == 1:
+        if slot == BEFORE:
             pl.semaphore_wait(barrier, len(partners))
-            for ready in range(1 + 1):
-                start(ready)
-        if slot > 1:
-            start(slot)
+            for first in range(slot - 1):
+                start(first)
+        if slot >= BEFORE:
+            start(slot - 1)
 
     for offset in SIDES + [ACROSS]:
         here.signal(plane_in, offset)

time: 34.4 us -> 34.4 us (level)
  no operation moved by 1% of the time
where the time goes in v7:
time: 34.4 us; the launch traced here: 34.3 us
  Pallas kernels  33 us (96%)
  between operations  1.28 us (4%)
    pallas_call x1, Pallas kernels, body(): pl.pallas_call(functools.partial(kernel, total_entries), out_shape=out_sh...  32.3 us

profile of v7, /device:TPU:1, one launch (start us, length us, event | category | flops | bytes accessed | tf_op | source)
XLA Modules:
  0.0 34.3 jit_solution(9434931968703340897)
XLA Ops:
  1.3 32.3 %krum.1 = (f32[16]{0:T(128)S(1)}, f32[256,128]{1,0:T(8,128)S(1)}) custom-call(s32[1]{0:T(128)S(6)} %copy.5.winner_ref, s32[16,11]{1,0:T(8,128)} %neighbours_hbm.1, f32[4096,128]{1,0:T(8,128)} %bitcast.2), custom_call_target="tpu_custom_call" | custom-call | tf_op jit(solution)/shard_map/krum/pallas_call | solution.py:273
  33.6 0.7 %finish.1 = (f32[16]{0:T(128)}, f32[256,128]{1,0:T(8,128)}) custom-call(f32[16]{0:T(128)S(1)} %get-tuple-element.6.scores_ref, f32[256,128]{1,0:T(8,128)S(1)} %get-tuple-element.7.block_ref), custom_call_target="tpu_custom_call" | custom-call | tf_op jit(solution)/shard_map/finish/pallas_call | solution.py:319
